TPU v7x, 32 devices: a whole 2x2x4 slice. The times are simulated.
32 devices in a mesh: gx: 8 (over y, x, core), gy: 4 (over z).
Axes of the slice: x: 2, y: 2, z: 4, core: 2. Of those that a mesh axis runs over, the one named last changes fastest.
Arguments:
- volts: float32 [32, 4, 64, 512], P(None, None, 'gx', 'gy'), may hold values from -6 to 6
- cap: float32 [4, 64, 512], P(None, 'gx', 'gy'), may hold values from 0.05 to 1
- cond_x: float32 [4, 64, 512], P(None, 'gx', 'gy'), may hold values from 0.5 to 2
- cond_y: float32 [4, 64, 512], P(None, 'gx', 'gy'), may hold values from 0.5 to 2
- via: float32 [4, 64, 512], P(None, 'gx', 'gy'), may hold values from 0.2 to 2
- waveforms: float32 [64, 64], replicated, may hold values from -6 to 6
- placement: int32 [262144, 1], P(('gx', 'gy')), may hold values from 0 to 31; in each aligned block of 8192 rows (0 to 8191, 8192 to 16383, ...) at most 512 rows name the same one
- cells: int32 [262144], P(('gx', 'gy')), may hold values from 0 to 1023
- wave_ids: int32 [262144], P(('gx', 'gy')), may hold values from 0 to 63
- amps: float32 [262144], P(('gx', 'gy')), may hold values from 0.5 to 4
Outputs:
- volts_out: float32 [32, 4, 64, 512], P(None, None, 'gx', 'gy')
- residual: float32 [32, 4, 64, 512], P(None, None, 'gx', 'gy')
Inputs may be any that keep to these rules, and one draw needn't show every extreme that they name: `placement`: in each device's block of 8192 rows no tile is named more than 512 times, a bound that some block reaches.
All inputs are finite; a program needn't handle non-finite values.
Results may differ from a plain program's by a relative error of at most 0.0029.
Values may be sent and summed in bfloat16 or wider, within the bound.
A program may use at most 64 MiB of HBM per device.

v0:
```python
import jax
import jax.numpy as jnp
from jax import lax
from jax.sharding import PartitionSpec as P

ITERS = 3


def with_halo(block, sides, width):
    for axis, dim in sides:
        count = lax.axis_size(axis)
        forward = [(i, i + 1) for i in range(count - 1)]
        backward = [(target, source) for source, target in forward]
        low = lax.ppermute(
            lax.slice_in_dim(block, block.shape[dim] - width, None, axis=dim), axis, forward
        )
        high = lax.ppermute(lax.slice_in_dim(block, 0, width, axis=dim), axis, backward)
        block = jnp.concatenate([low, block, high], axis=dim)
    return block


def shifted(x, axis, by):
    length = lax.axis_size(axis)
    pairs = [(i, i + by) for i in range(length) if 0 <= i + by < length]
    return lax.ppermute(x, axis, pairs)


def gram(left, right):
    left_rows = left.reshape(left.shape[0], -1)
    right_rows = right.reshape(right.shape[0], -1)
    return lax.dot_general(
        left_rows, right_rows, (((1,), (1,)), ((), ())), precision=lax.Precision.HIGHEST
    )


def combine(coef, field):
    return jnp.einsum("st,slxy->tlxy", coef, field, precision=lax.Precision.HIGHEST)


def spd_solve(matrix, right):
    factor = jnp.linalg.cholesky(matrix)
    return jax.scipy.linalg.cho_solve((factor, True), right)


def make_currents(waveforms, kinds, scales):
    table_hits = (
        jnp.arange(waveforms.shape[1], dtype=jnp.int32)[:, None] == kinds[None, :]
    ).astype(jnp.float32)
    picked = jnp.dot(waveforms, table_hits, precision=lax.Precision.HIGHEST)
    return (picked * scales[None, :]).astype(jnp.bfloat16)


def operate(field, cap, cond_x, cond_x_low, cond_y, cond_y_low, via, via_low):
    padded = with_halo(field, (("gx", 2), ("gy", 3)), 1)
    zero_layer = jnp.zeros_like(field[:, :1])
    upper = jnp.concatenate([field[:, 1:], zero_layer], axis=1)
    lower = jnp.concatenate([zero_layer, field[:, :-1]], axis=1)
    result = cap * field
    result = result + cond_x * (field - padded[:, :, 2:, 1:-1])
    result = result + cond_x_low * (field - padded[:, :, :-2, 1:-1])
    result = result + cond_y * (field - padded[:, :, 1:-1, 2:])
    result = result + cond_y_low * (field - padded[:, :, 1:-1, :-2])
    result = result + via * (field - upper) + via_low * (field - lower)
    return result


def body(volts, cap, cond_x, cond_y, via, waveforms, placement, cells, wave_ids, amps):
    devices = lax.axis_size(("gx", "gy"))
    scenarios = volts.shape[0]
    steps = waveforms.shape[0] // scenarios
    tile_x = volts.shape[2]
    tile_y = volts.shape[3]
    die_cells = tile_x * tile_y
    slots_all = 2 * cells.shape[0]
    capacity = slots_all // devices
    target = placement[:, 0]
    target_hits = (jnp.arange(devices, dtype=jnp.int32)[:, None] == target[None, :]).astype(
        jnp.int32
    )
    running = jnp.cumsum(target_hits, axis=1) - 1
    position = jnp.sum(target_hits * running, axis=0)
    slot_index = target * capacity + position
    currents = make_currents(waveforms, wave_ids, amps)
    packed = jnp.zeros((currents.shape[0], slots_all), jnp.bfloat16).at[:, slot_index].set(currents)
    cell_slots = jnp.zeros((1, slots_all), jnp.int32).at[0, slot_index].set(cells)
    arrived, cell_slots = (
        lax.all_to_all(packed, ("gx", "gy"), split_axis=1, concat_axis=1, tiled=True),
        lax.all_to_all(cell_slots, ("gx", "gy"), split_axis=1, concat_axis=1, tiled=True),
    )
    block_rows = min(1024, slots_all)
    block_count = slots_all // block_rows
    cell_line = jnp.arange(die_cells, dtype=jnp.int32)

    def add_block(turn, total):
        piece_values = lax.dynamic_slice_in_dim(arrived, turn * block_rows, block_rows, 1)
        piece_cells = lax.dynamic_slice_in_dim(cell_slots[0], turn * block_rows, block_rows, 0)
        one_hot = (piece_cells[:, None] == cell_line[None, :]).astype(jnp.bfloat16)
        return total + jnp.dot(piece_values, one_hot, preferred_element_type=jnp.float32)

    injected = lax.fori_loop(
        0, block_count, add_block, jnp.zeros((arrived.shape[0], die_cells), jnp.float32)
    )
    injected = injected.reshape(steps, scenarios, tile_x, tile_y)
    rim_x = shifted(cond_x[:, -1:, :], "gx", 1)
    rim_y = shifted(cond_y[:, :, -1:], "gy", 1)
    cond_x_low = jnp.concatenate([rim_x, cond_x[:, :-1, :]], axis=1)
    cond_y_low = jnp.concatenate([rim_y, cond_y[:, :, :-1]], axis=2)
    via_low = jnp.concatenate([jnp.zeros_like(via[:1]), via[:-1]], axis=0)

    def apply_grid(field):
        return operate(field, cap, cond_x, cond_x_low, cond_y, cond_y_low, via, via_low)

    voltage = volts
    residual = volts
    for step in range(steps):
        rhs = cap * voltage
        rhs = rhs.at[:, 0].add(-injected[step])
        iterate = voltage
        residual = rhs - apply_grid(iterate)
        direction = residual
        norm_gram = lax.psum(gram(residual, residual), ("gx", "gy"))
        for sweep in range(ITERS):
            image = apply_grid(direction)
            curve_gram, cross_gram, image_gram = lax.psum(
                (gram(direction, image), gram(residual, image), gram(image, image)), ("gx", "gy")
            )
            step_coef = spd_solve(curve_gram, norm_gram)
            iterate = iterate + combine(step_coef, direction)
            residual = residual - combine(step_coef, image)
            if sweep + 1 < ITERS:
                cross_term = jnp.dot(cross_gram, step_coef, precision=lax.Precision.HIGHEST)
                square_term = jnp.dot(
                    step_coef.T,
                    jnp.dot(image_gram, step_coef, precision=lax.Precision.HIGHEST),
                    precision=lax.Precision.HIGHEST,
                )
                new_gram = norm_gram - cross_term - cross_term.T + square_term
                turn_coef = spd_solve(norm_gram, new_gram)
                direction = residual + combine(turn_coef, direction)
                norm_gram = new_gram
        voltage = iterate
    return (voltage, residual)


def solution(mesh):
    return jax.shard_map(
        body,
        mesh=mesh,
        in_specs=(
            P(None, None, "gx", "gy"),
            P(None, "gx", "gy"),
            P(None, "gx", "gy"),
            P(None, "gx", "gy"),
            P(None, "gx", "gy"),
            P(),
            P(("gx", "gy"), None),
            P(("gx", "gy")),
            P(("gx", "gy")),
            P(("gx", "gy")),
        ),
        out_specs=(P(None, None, "gx", "gy"), P(None, None, "gx", "gy")),
        check_vma=False,
    )
```

profile of v0, /device:TPU:0, one launch (start us, length us, event | category | flops | bytes accessed | tf_op | source)
XLA Modules:
  0.0 647.6 jit_solution(1546838298687216187)
XLA Ops:
  1.6 9.5 %reduce-window.6 = s32[32,64,128]{2,1,0:T(8,128)S(1)} reduce-window(s32[32,64,128]{2,1,0:T(8,128)S(1)} %fusion.11, s32[]{:T(128)} %constant.128.clone.1), window={size=1x1x128 pad=0_0x0_0x127_0}, to_apply=%region_0.0 | reduce-window | flops 33292288 | bytes 2097156 | tf_op jit(solution)/shard_map/reduce-window
  14.9 23.7 %scatter_custom_fusion = bf16[64,16384]{0,1:T(8,128)(2,1)} fusion(s32[8192]{0:T(1024)S(1)} %bitcast.343, bf16[8192,64]{1,0:T(8,128)(2,1)S(1)} %copy.219, bf16[]{:T(256)} %constant.130.clone.1), kind=kCustom, calls=%fused_computation.13 | custom fusion | bytes 2097154 | tf_op jit(solution)/shard_map/scatter | solution.py:84
  38.6 4.8 copy.220
  43.3 7.3 %all-to-all-start = ((bf16[64,32,512]{2,0,1:T(8,128)(2,1)}), bf16[64,32,512]{2,0,1:T(8,128)(2,1)S(1)}, u32[]{:S(2)}, u32[]{:S(2)}) async-start(bf16[64,32,512]{2,0,1:T(8,128)(2,1)} %copy.220), calls=%async_computation | async-start | bytes 4194304 | tf_op jit(solution)/shard_map/all_to_all | solution.py:87
  55.2 3.5 collective-permute-start.4
  58.8 3.7 collective-permute-start.1
  62.9 31.2 %scatter_custom_fusion.1 = s32[16384]{0:T(1024)} fusion(s32[8192]{0:T(1024)S(1)} %broadcast_select_fusion, s32[8192]{0:T(1024)} %param.26, s32[]{:T(128)} %constant.128.clone.1), kind=kCustom, calls=%fused_computation.270 | custom fusion | bytes 66048
  97.6 7.3 %all-to-all-start.1 = ((s32[1,32,512]{2,0,1:T(1,128)}), s32[1,32,512]{2,0,1:T(1,128)}, u32[]{:S(2)}, u32[]{:S(2)}) async-start(s32[1,32,512]{2,0,1:T(1,128)} %bitcast.344), calls=%async_computation.1 | async-start | bytes 131072 | tf_op jit(solution)/shard_map/all_to_all | solution.py:88
  110.3 5.0 collective-permute-start.5
  119.2 53.7 %while.16 = (s32[]{:T(128)}, f32[64,1024]{1,0:T(8,128)}, bf16[64,16384]{1,0:T(8,128)(2,1)}, s32[1,16384]{1,0:T(1,128)}, s32[]{:T(128)}, /*index=5*/s32[]{:T(128)}, s32[]{:T(128)}, s32[]{:T(128)}) while((s32[]{:T(128)}, f32[64,1024]{1,0:T(8,128)}, bf16[64,16384]{1,0:T(8,128)(2,1)}, s32[1,16384]{1,0:T(1,128)}, s32[]{:T(128)}, ...), condition=%wide.region_6.7_spmd.clone, body=%wide.region_5.6_spmd.clone.sunk | while | flops 135397376 | bytes 667797 | solution.py:100
  177.8 3.0 collective-permute-start.7
  184.0 4.6 collective-permute-start.9
  192.3 44.5 %all-reduce.21 = (f32[32,32]{0,1:T(8,128)S(1)}, f32[32,32]{0,1:T(8,128)S(1)}, f32[32,32]{1,0:T(8,128)S(1)}) all-reduce(f32[32,32]{0,1:T(8,128)S(1)} %convolution_bitcast_fusion.18, f32[32,32]{0,1:T(8,128)S(1)} %convolution_bitcast_fusion.19, f32[32,32]{1,0:T(8,128)S(1)} %convolution_bitcast_fusion.17), channel_id=1, replica_groups=mesh['gx'=8,'gy'=4] {'gx','gy'}, use_global_device_ids=true, to_apply=%region_10.12 | all-reduce | flops 3072 | bytes 24576 | tf_op jit(solution)/shard_map/psum | solution.py:121
  259.2 3.0 collective-permute-start.11
  266.5 4.7 collective-permute-start.13
  271.9 3.1 custom-call.20
  279.1 43.3 %all-reduce.20 = (f32[32,32]{0,1:T(8,128)S(1)}, f32[32,32]{1,0:T(8,128)S(1)}, f32[32,32]{1,0:T(8,128)S(1)}) all-reduce(f32[32,32]{0,1:T(8,128)S(1)} %convolution_bitcast_fusion.15, f32[32,32]{1,0:T(8,128)S(1)} %convolution_bitcast_fusion.13, f32[32,32]{1,0:T(8,128)S(1)} %convolution_bitcast_fusion.14), channel_id=1, replica_groups=mesh['gx'=8,'gy'=4] {'gx','gy'}, use_global_device_ids=true, to_apply=%region_12.15 | all-reduce | flops 3072 | bytes 24576 | tf_op jit(solution)/shard_map/psum | solution.py:124
  333.2 3.0 collective-permute-start.15
  340.3 4.5 collective-permute-start.17
  347.7 43.9 %psum.110 = f32[32,32]{0,1:T(8,128)S(1)} all-reduce(f32[32,32]{0,1:T(8,128)S(1)} %convolution_bitcast_fusion.11), channel_id=1, replica_groups=mesh['gx'=8,'gy'=4] {'gx','gy'}, use_global_device_ids=true, to_apply=%region_15.18 | all-reduce | flops 1024 | bytes 8192 | tf_op jit(solution)/shard_map/psum | solution.py:124
  400.7 3.0 collective-permute-start.19
  408.1 4.8 collective-permute-start.21
  417.4 3.3 collective-permute-start.23
  425.0 4.6 collective-permute-start.25
  434.2 46.8 %all-reduce.19 = (f32[32,32]{0,1:T(8,128)S(1)}, f32[32,32]{0,1:T(8,128)S(1)}, f32[32,32]{1,0:T(8,128)S(1)}) all-reduce(f32[32,32]{0,1:T(8,128)S(1)} %convolution_bitcast_fusion.8, f32[32,32]{0,1:T(8,128)S(1)} %convolution_bitcast_fusion.9, f32[32,32]{1,0:T(8,128)S(1)} %convolution_bitcast_fusion.7), channel_id=1, replica_groups=mesh['gx'=8,'gy'=4] {'gx','gy'}, use_global_device_ids=true, to_apply=%region_17.20 | all-reduce | flops 3072 | bytes 24576 | tf_op jit(solution)/shard_map/psum | solution.py:121
  504.1 3.0 collective-permute-start.27
  510.2 4.8 collective-permute-start.29
  515.7 3.1 custom-call.25
  522.7 42.7 %all-reduce.18 = (f32[32,32]{0,1:T(8,128)S(1)}, f32[32,32]{1,0:T(8,128)S(1)}, f32[32,32]{1,0:T(8,128)S(1)}) all-reduce(f32[32,32]{0,1:T(8,128)S(1)} %convolution_bitcast_fusion.5, f32[32,32]{1,0:T(8,128)S(1)} %convolution_bitcast_fusion.3, f32[32,32]{1,0:T(8,128)S(1)} %convolution_bitcast_fusion.4), channel_id=1, replica_groups=mesh['gx'=8,'gy'=4] {'gx','gy'}, use_global_device_ids=true, to_apply=%region_19.22 | all-reduce | flops 3072 | bytes 24576 | tf_op jit(solution)/shard_map/psum | solution.py:124
  576.2 3.0 collective-permute-start.31
  583.3 4.5 collective-permute-start.33
  592.1 44.5 %psum.117 = f32[32,32]{0,1:T(8,128)S(1)} all-reduce(f32[32,32]{0,1:T(8,128)S(1)} %convolution_bitcast_fusion.1), channel_id=1, replica_groups=mesh['gx'=8,'gy'=4] {'gx','gy'}, use_global_device_ids=true, to_apply=%region_22.25 | all-reduce | flops 1024 | bytes 8192 | tf_op jit(solution)/shard_map/psum | solution.py:124
  (389 shorter events, 223.1 us)
Async XLA Ops:
  43.3 54.2 %all-to-all-start = ((bf16[64,32,512]{2,0,1:T(8,128)(2,1)}), bf16[64,32,512]{2,0,1:T(8,128)(2,1)S(1)}, u32[]{:S(2)}, u32[]{:S(2)}) async-start(bf16[64,32,512]{2,0,1:T(8,128)(2,1)} %copy.220), calls=%async_computation | async-start | bytes 4194304 | tf_op jit(solution)/shard_map/all_to_all | solution.py:87
  51.7 43.5 %collective-permute-start.2 = (f32[32,4,1,128]{3,0,2,1:T(8,128)S(1)}, f32[32,4,1,128]{3,0,2,1:T(8,128)S(1)}, u32[]{:S(2)}, u32[]{:S(2)}) collective-permute-start(f32[32,4,1,128]{3,0,2,1:T(8,128)S(1)} %get-tuple-element.215), channel_id=1, source_target_pairs={{0,4},{4,8},{8,12},{12,16},{16,20},{20,24},{24,28},{1,5},{5,9},{9,... | collective-permute-start | bytes 196616 | tf_op jit(solution)/shard_map/ppermute | solution.py:14
  53.8 43.6 %collective-permute-start = (f32[32,4,1,128]{3,0,2,1:T(8,128)}, f32[32,4,1,128]{3,0,2,1:T(8,128)S(1)}, u32[]{:S(2)}, u32[]{:S(2)}) collective-permute-start(f32[32,4,1,128]{3,0,2,1:T(8,128)} %get-tuple-element.214), channel_id=1, source_target_pairs={{4,0},{8,4},{12,8},{16,12},{20,16},{24,20},{28,24},{5,1},{9,5},{13... | collective-permute-start | bytes 196616 | tf_op jit(solution)/shard_map/ppermute | solution.py:17
  55.2 39.9 %collective-permute-start.4 = (f32[4,8,1]{2,1,0:T(8,128)S(1)}, f32[4,8,1]{2,1,0:T(8,128)S(1)}, u32[]{:S(2)}, u32[]{:S(2)}) collective-permute-start(f32[4,8,1]{2,1,0:T(8,128)S(1)} %slice.379), channel_id=1, source_target_pairs={{0,1},{1,2},{2,3},{4,5},{5,6},{6,7},{8,9},{9,10},{10,11},{12,13},{... | collective-permute-start | bytes 392 | tf_op jit(solution)/shard_map/ppermute | solution.py:25
  58.8 56.5 %collective-permute-start.1 = (f32[4,1,128]{2,1,0:T(1,128)S(1)}, f32[4,1,128]{2,1,0:T(1,128)S(1)}, u32[]{:S(2)}, u32[]{:S(2)}) collective-permute-start(f32[4,1,128]{2,1,0:T(1,128)S(1)} %slice.373), channel_id=1, source_target_pairs={{0,4},{4,8},{8,12},{12,16},{16,20},{20,24},{24,28},{1,5},{5,9},{9,... | collective-permute-start | bytes 6152 | tf_op jit(solution)/shard_map/ppermute | solution.py:25
  97.6 21.6 %all-to-all-start.1 = ((s32[1,32,512]{2,0,1:T(1,128)}), s32[1,32,512]{2,0,1:T(1,128)}, u32[]{:S(2)}, u32[]{:S(2)}) async-start(s32[1,32,512]{2,0,1:T(1,128)} %bitcast.344), calls=%async_computation.1 | async-start | bytes 131072 | tf_op jit(solution)/shard_map/all_to_all | solution.py:88
  107.6 7.7 %collective-permute-start.3 = (f32[32,4,10,1]{0,1,3,2:T(4,128)S(1)}, f32[32,4,10,1]{0,1,3,2:T(4,128)S(1)}, u32[]{:S(2)}, u32[]{:S(2)}) collective-permute-start(f32[32,4,10,1]{0,1,3,2:T(4,128)S(1)} %copy.230), channel_id=1, source_target_pairs={{1,0},{2,1},{3,2},{5,4},{6,5},{7,6},{9,8},{10,9},{11,10},{13,12},{... | collective-permute-start | bytes 15368 | tf_op jit(solution)/shard_map/ppermute | solution.py:17
  110.3 6.2 collective-permute-start.5
  176.5 4.4 collective-permute-start.6
  182.4 7.5 %collective-permute-start.8 = (f32[32,4,10,1]{0,1,3,2:T(4,128)S(1)}, f32[32,4,10,1]{0,1,3,2:T(4,128)S(1)}, u32[]{:S(2)}, u32[]{:S(2)}) collective-permute-start(f32[32,4,10,1]{0,1,3,2:T(4,128)S(1)} %copy.240), channel_id=1, source_target_pairs={{1,0},{2,1},{3,2},{5,4},{6,5},{7,6},{9,8},{10,9},{11,10},{13,12},{... | collective-permute-start | bytes 15368 | tf_op jit(solution)/shard_map/ppermute | solution.py:17
  184.0 6.2 collective-permute-start.9
  257.9 5.1 collective-permute-start.10
  259.2 3.9 collective-permute-start.11
  264.9 10.1 %collective-permute-start.12 = (f32[32,4,10,1]{0,1,3,2:T(4,128)S(1)}, f32[32,4,10,1]{0,1,3,2:T(4,128)S(1)}, u32[]{:S(2)}, u32[]{:S(2)}) collective-permute-start(f32[32,4,10,1]{0,1,3,2:T(4,128)S(1)} %copy.254), channel_id=1, source_target_pairs={{1,0},{2,1},{3,2},{5,4},{6,5},{7,6},{9,8},{10,9},{11,10},{13,12},{... | collective-permute-start | bytes 15368 | tf_op jit(solution)/shard_map/ppermute | solution.py:17
  266.5 8.8 %collective-permute-start.13 = (f32[32,4,10,1]{0,1,3,2:T(4,128)S(1)}, f32[32,4,10,1]{0,1,3,2:T(4,128)S(1)}, u32[]{:S(2)}, u32[]{:S(2)}) collective-permute-start(f32[32,4,10,1]{0,1,3,2:T(4,128)S(1)} %copy.256), channel_id=1, source_target_pairs={{0,1},{1,2},{2,3},{4,5},{5,6},{6,7},{8,9},{9,10},{10,11},{12,13},{... | collective-permute-start | bytes 15368 | tf_op jit(solution)/shard_map/ppermute | solution.py:14
  331.9 5.0 collective-permute-start.14
  333.2 3.9 collective-permute-start.15
  338.7 6.3 collective-permute-start.16
  340.3 6.0 collective-permute-start.17
  399.4 5.2 collective-permute-start.18
  406.5 6.4 collective-permute-start.20
  408.1 6.0 collective-permute-start.21
  416.1 5.4 collective-permute-start.22
  417.4 4.2 collective-permute-start.23
  423.4 6.7 %collective-permute-start.24 = (f32[32,4,10,1]{0,1,3,2:T(4,128)S(1)}, f32[32,4,10,1]{0,1,3,2:T(4,128)S(1)}, u32[]{:S(2)}, u32[]{:S(2)}) collective-permute-start(f32[32,4,10,1]{0,1,3,2:T(4,128)S(1)} %copy.278), channel_id=1, source_target_pairs={{1,0},{2,1},{3,2},{5,4},{6,5},{7,6},{9,8},{10,9},{11,10},{13,12},{... | collective-permute-start | bytes 15368 | tf_op jit(solution)/shard_map/ppermute | solution.py:17
  425.0 6.0 collective-permute-start.25
  502.8 5.0 collective-permute-start.26
  508.6 10.1 %collective-permute-start.28 = (f32[32,4,10,1]{0,1,3,2:T(4,128)S(1)}, f32[32,4,10,1]{0,1,3,2:T(4,128)S(1)}, u32[]{:S(2)}, u32[]{:S(2)}) collective-permute-start(f32[32,4,10,1]{0,1,3,2:T(4,128)S(1)} %copy.291), channel_id=1, source_target_pairs={{1,0},{2,1},{3,2},{5,4},{6,5},{7,6},{9,8},{10,9},{11,10},{13,12},{... | collective-permute-start | bytes 15368 | tf_op jit(solution)/shard_map/ppermute | solution.py:17
  510.2 8.8 %collective-permute-start.29 = (f32[32,4,10,1]{0,1,3,2:T(4,128)S(1)}, f32[32,4,10,1]{0,1,3,2:T(4,128)S(1)}, u32[]{:S(2)}, u32[]{:S(2)}) collective-permute-start(f32[32,4,10,1]{0,1,3,2:T(4,128)S(1)} %copy.293), channel_id=1, source_target_pairs={{0,1},{1,2},{2,3},{4,5},{5,6},{6,7},{8,9},{9,10},{10,11},{12,13},{... | collective-permute-start | bytes 15368 | tf_op jit(solution)/shard_map/ppermute | solution.py:14
  574.9 5.0 collective-permute-start.30
  581.7 7.1 %collective-permute-start.32 = (f32[32,4,10,1]{0,1,3,2:T(4,128)S(1)}, f32[32,4,10,1]{0,1,3,2:T(4,128)S(1)}, u32[]{:S(2)}, u32[]{:S(2)}) collective-permute-start(f32[32,4,10,1]{0,1,3,2:T(4,128)S(1)} %copy.303), channel_id=1, source_target_pairs={{1,0},{2,1},{3,2},{5,4},{6,5},{7,6},{9,8},{10,9},{11,10},{13,12},{... | collective-permute-start | bytes 15368 | tf_op jit(solution)/shard_map/ppermute | solution.py:17
  583.3 6.0 collective-permute-start.33
  (41 other events, 692.0 us)
where the time goes:
time: 658 us; the launch traced here: 648 us
  blocking collectives  266 us (40%)
  local copies, waits for them, and re-layouts  107 us (16%)
  starting transfers between devices  104 us (16%)
  other arithmetic  95.1 us (14%)
  matrix products  68.5 us (10%)
    psum x4, blocking collectives, body(): lax.psum((gram(direction, image), gram(residual, image), gram(image, imag...  174 us
    psum x2, blocking collectives, body(): norm_gram = lax.psum(gram(residual, residual), ('gx', 'gy'))  91.3 us
    ppermute x16, starting transfers between devices, with_halo(): lax.ppermute(lax.slice_in_dim(block, block.shape[dim] - width, None, axis...  61.2 us
    dot_general x16, matrix products, add_block(): jnp.dot(piece_values, one_hot, preferred_element_type=jnp.float32)  42.7 us
    unnamed x79, local copies, waits for them, and re-layouts  40.2 us
    another operation x30, other arithmetic, spd_solve(): factor = jnp.linalg.cholesky(matrix)  36.1 us
    another operation x20, other arithmetic, spd_solve(): return jax.scipy.linalg.cho_solve((factor, True), right)  32.2 us
    scatter x1, local copies, waits for them, and re-layouts, body(): jnp.zeros((currents.shape[0], slots_all), jnp.bfloat16).at[:, slot_index]  23.7 us
  transfers between devices with their start and end apart: 36, of which 10 were waited for; matrix products, arithmetic and copies ran while one was open for 10% of the time, Pallas kernels for 0%

commit v1 on v0

v1 whole, which is shorter than its diff:
```python
import functools

import jax
import jax.numpy as jnp
from jax import lax
from jax.experimental import pallas as pl
from jax.experimental.pallas import tpu as pltpu
from jax.sharding import PartitionSpec as P

ITERS = 3
LANES = 128
MESH = pl.DeviceIdType.MESH
HIGHEST = lax.Precision.HIGHEST
NT = (((1,), (1,)), ((), ()))
TN = (((0,), (0,)), ((), ()))
F32 = jnp.float32
BF16 = jnp.bfloat16


def split3(x):
    first = x.astype(BF16).astype(F32)
    rest = x - first
    second = rest.astype(BF16).astype(F32)
    return first, second, rest - second


def rows_iota(rows, cols):
    return lax.broadcasted_iota(jnp.int32, (rows, cols), 0)


def bin_kernel(devices, capacity, target_ref, cell_ref, wave_ref, amp_ref, out_ref, acc_ref):
    blocks, width = target_ref.shape
    rows = out_ref.shape[1]
    before = (
        rows_iota(width, width) < lax.broadcasted_iota(jnp.int32, (width, width), 1)
    ).astype(F32).astype(BF16)
    acc_ref[...] = jnp.zeros_like(acc_ref)

    def step(b, base):
        target = target_ref[pl.ds(b, 1), :]
        hits = (rows_iota(devices, width) == target).astype(F32)
        ahead = jnp.dot(hits.astype(BF16), before, preferred_element_type=F32)
        position = jnp.sum(hits * (ahead + base), axis=0, keepdims=True)
        slot = target * capacity + position.astype(jnp.int32)
        row_hits = rows_iota(rows, width) == (slot >> 7)
        lane_hits = (rows_iota(LANES, width) == (slot & 127)).astype(F32).astype(BF16)
        code = cell_ref[pl.ds(b, 1), :] * 64 + wave_ref[pl.ds(b, 1), :]
        parts = split3(amp_ref[pl.ds(b, 1), :]) + (
            (code >> 8).astype(F32),
            (code & 255).astype(F32),
        )
        for i, part in enumerate(parts):
            left = jnp.where(row_hits, part, 0.0).astype(BF16)
            acc_ref[i] += lax.dot_general(left, lane_hits, NT, preferred_element_type=F32)
        return base + jnp.sum(hits, axis=1, keepdims=True)

    lax.fori_loop(0, blocks, step, jnp.zeros((devices, 1), F32), unroll=2)
    out_ref[0] = (acc_ref[2] + acc_ref[1]) + acc_ref[0]
    out_ref[1] = acc_ref[3] * 256.0 + acc_ref[4]


def bin_instances(devices, capacity, target, cells, wave_ids, amps):
    width = 512
    shape = (target.shape[0] // width, width)
    rows = devices * capacity // LANES
    return pl.pallas_call(
        functools.partial(bin_kernel, devices, capacity),
        out_shape=jax.ShapeDtypeStruct((2, rows, LANES), F32),
        in_specs=[pl.BlockSpec(memory_space=pltpu.VMEM)] * 4,
        out_specs=pl.BlockSpec(memory_space=pltpu.VMEM),
        scratch_shapes=[pltpu.VMEM((5, rows, LANES), F32)],
        name="bin",
    )(*[x.reshape(shape) for x in (target, cells, wave_ids, amps)])


def inject_kernel(parts, arrived_ref, wave_ref, out_ref, acc_ref):
    sources, width = arrived_ref.shape[1:]
    kinds = wave_ref.shape[1]
    outs = wave_ref.shape[0]
    low_count = out_ref.shape[1] // parts
    table = jnp.concatenate(split3(wave_ref[...]), axis=0).astype(BF16)
    acc_ref[...] = jnp.zeros_like(acc_ref)

    def step(i, carry):
        amp = arrived_ref[0, pl.ds(i, 1), :]
        code = arrived_ref[1, pl.ds(i, 1), :].astype(jnp.int32)
        cell = code >> 6
        low, high = cell % low_count, cell // low_count
        kind_hits = (rows_iota(kinds, width) == (code & 63)).astype(F32).astype(BF16)
        picked = jnp.dot(table, kind_hits, preferred_element_type=F32)
        wave = (picked[2 * outs :] + picked[outs : 2 * outs]) + picked[:outs]
        currents = (wave * amp).astype(BF16).astype(F32)
        low_hits = (rows_iota(low_count, width) == low).astype(F32).astype(BF16)
        left = jnp.concatenate(
            [jnp.where(high == h, currents, 0.0).astype(BF16) for h in range(parts)], axis=0
        )
        acc_ref[...] += lax.dot_general(left, low_hits, NT, preferred_element_type=F32)
        return carry

    lax.fori_loop(0, sources, step, 0, unroll=2)
    for h in range(parts):
        out_ref[:, h * low_count : (h + 1) * low_count] = acc_ref[h * outs : (h + 1) * outs]


def inject(arrived, waveforms, die_cells):
    parts = 4
    return pl.pallas_call(
        functools.partial(inject_kernel, parts),
        out_shape=jax.ShapeDtypeStruct((waveforms.shape[0], die_cells), F32),
        in_specs=[pl.BlockSpec(memory_space=pltpu.VMEM)] * 2,
        out_specs=pl.BlockSpec(memory_space=pltpu.VMEM),
        scratch_shapes=[pltpu.VMEM((parts * waveforms.shape[0], die_cells // parts), F32)],
        name="inject",
    )(arrived, waveforms)


def eliminate(mats):
    size = mats[0].shape[0]
    rows = rows_iota(size, mats[0].shape[1])
    for k in range(size):
        fresh = []
        for m in mats:
            row = m[k : k + 1, :] / m[k : k + 1, k : k + 1]
            fresh.append(jnp.where(rows == k, row, m - m[:, k : k + 1] * row))
        mats = fresh
    return mats


def beside(left, right):
    size = left.shape[0]
    return jnp.concatenate([left, right, jnp.zeros((size, LANES - 2 * size), F32)], axis=1)


def small(a, b, dims=(((1,), (0,)), ((), ()))):
    return lax.dot_general(a, b, dims, precision=HIGHEST, preferred_element_type=F32)


def grid_kernel(
    nx, ny, steps, layers, tile_x,
    v_in, inj, coef, v, r,
    d, image, xs, xl, ys, yl, gs, gl, hs, hl,
    xsend, xrecv, ysend, yrecv, gsend, grecv, hsend, hrecv,
):
    gx, gy = lax.axis_index("gx"), lax.axis_index("gy")
    size = v.shape[0]
    count = layers * tile_x
    lane = lax.broadcasted_iota(jnp.int32, (size, LANES), 1)

    barrier = pltpu.get_barrier_semaphore()
    for axis, me, n in (("gx", gx, nx), ("gy", gy, ny)):
        for j in range(1, n):
            pl.semaphore_signal(
                barrier, inc=1, device_id={axis: lax.rem(me + j, n)}, device_id_type=MESH
            )
    pl.semaphore_wait(barrier, nx + ny - 2)

    def block(ref, c):
        return ref[:, c * LANES : (c + 1) * LANES]

    def exchange(src, e):
        for l in range(layers):
            at = slice(l * LANES, (l + 1) * LANES)
            xs[e, 0, :, at] = block(src, l * tile_x + tile_x - 1)
            xs[e, 1, :, at] = block(src, l * tile_x)
        copies = []
        for side, step in ((0, 1), (1, nx - 1)):
            copies.append(pltpu.make_async_remote_copy(
                xs.at[e, side], xl.at[e, side], xsend.at[e, side], xrecv.at[e, side],
                device_id={"gx": lax.rem(gx + step, nx)}, device_id_type=MESH,
            ))
            copies[-1].start()
        last = jnp.zeros((size, LANES), F32)
        first = last
        for c in range(count):
            f = block(src, c)
            last = jnp.where(lane == c, pltpu.roll(f, (c + 1) % LANES, 1), last)
            first = jnp.where(lane == c, pltpu.roll(f, c, 1) if c else f, first)
        ys[e, 0] = last
        ys[e, 1] = first
        for side, step in ((0, 1), (1, ny - 1)):
            copies.append(pltpu.make_async_remote_copy(
                ys.at[e, side], yl.at[e, side], ysend.at[e, side], yrecv.at[e, side],
                device_id={"gy": lax.rem(gy + step, ny)}, device_id_type=MESH,
            ))
            copies[-1].start()
        for copy in copies:
            copy.wait()

    def stencil(src, e, own, dst, finish):
        y_low, y_high = yl[e, 0], yl[e, 1]
        for c in range(count):
            l, x = divmod(c, tile_x)
            f = block(src, c)
            at = slice(l * LANES, (l + 1) * LANES)

            def k(i):
                return coef[i, c : c + 1, :]

            high = block(src, c + 1) if x + 1 < tile_x else xl[e, 1, :, at]
            low = block(src, c - 1) if x else xl[e, 0, :, at]
            total = k(own) * f - k(2) * high - k(3) * low
            after = jnp.where(
                lane == LANES - 1, pltpu.roll(y_high, LANES - 1 - c, 1), pltpu.roll(f, LANES - 1, 1)
            )
            ahead = jnp.where(
                lane == 0, pltpu.roll(y_low, LANES - c, 1) if c else y_low, pltpu.roll(f, 1, 1)
            )
            total = total - k(4) * after - k(5) * ahead
            if l + 1 < layers:
                total = total - k(6) * block(src, c + tile_x)
            if l:
                total = total - k(7) * block(src, c - tile_x)
            dst[:, c * LANES : (c + 1) * LANES] = finish(c, total)

    def start_all(send, land, e, ssem, rsem, axis, me, n):
        copies = []
        for j in range(1, n):
            copies.append(pltpu.make_async_remote_copy(
                send.at[e], land.at[e, j], ssem.at[e, j], rsem.at[e, j],
                device_id={axis: lax.rem(me + j, n)}, device_id_type=MESH,
            ))
            copies[-1].start()
        return copies

    def finish_all(copies, own, land, e, n):
        for copy in copies:
            copy.wait()
        total = own
        for j in range(1, n):
            total = total + land[e, j]
        return total

    def update(dst, base, coefs, field, sign):
        for c in range(layers):
            at = slice(c * tile_x * LANES, (c + 1) * tile_x * LANES)
            term = small(coefs, field[:, at], TN)
            dst[:, at] = base[:, at] + term if sign > 0 else base[:, at] - term

    v[...] = v_in[...]
    eye = (rows_iota(size, size) == lax.broadcasted_iota(jnp.int32, (size, size), 1)).astype(F32)
    pad = jnp.zeros((size, LANES - 3 * size), F32)

    def time_step(step, carry):
        e = step * (ITERS + 1)
        exchange(v, e)

        def residual_of(c, total):
            if c < tile_x:
                total = total + inj[pl.ds(pl.multiple_of(step * size, size), size),
                                    c * LANES : (c + 1) * LANES]
            return -total

        stencil(v, e, 1, r, residual_of)
        norm = None
        for sweep in range(ITERS):
            direction = d if sweep else r
            e = step * (ITERS + 1) + sweep + 1
            g = step * ITERS + sweep
            exchange(direction, e)
            stencil(direction, e, 0, image, lambda c, total: total)
            curve = small(direction[...], image[...], NT)
            if sweep + 1 < ITERS:
                square = small(image[...], image[...], NT)
                other = small(r[...], image[...] if sweep else r[...], NT)
                own = jnp.concatenate([curve, other, square, pad], axis=1)
            else:
                own = jnp.concatenate([curve, jnp.zeros((size, LANES - size), F32)], axis=1)
            gs[g] = own
            copies = start_all(gs, gl, g, gsend, grecv, "gx", gx, nx)
            inverse = None
            if sweep and sweep + 1 < ITERS:
                (inverse,) = eliminate([beside(norm, eye)])
            own = finish_all(copies, own, gl, g, nx)
            hs[g] = own
            copies = start_all(hs, hl, g, hsend, hrecv, "gy", gy, ny)
            total = finish_all(copies, own, hl, g, ny)
            curve = total[:, :size]
            cross = total[:, size : 2 * size]
            square = total[:, 2 * size : 3 * size]
            if sweep == 0:
                norm, cross = cross, curve
                solved, inverse = eliminate([beside(curve, norm), beside(norm, eye)])
            else:
                (solved,) = eliminate([beside(curve, norm)])
            step_coef = solved[:, size : 2 * size]
            update(v, v, step_coef, direction, 1)
            update(r, r, step_coef, image, -1) if sweep else None
            if sweep + 1 < ITERS:
                cross_term = small(cross, step_coef)
                cross_flip = small(step_coef, cross, (((0,), (1,)), ((), ())))
                square_term = small(step_coef, small(square, step_coef), TN)
                new = norm - cross_term - cross_flip + square_term
                turn = small(inverse[:, size : 2 * size], new)
                if sweep:
                    update(d, r, turn, d, 1)
                else:
                    update(d, r, turn, r, 1)
                    update(d, d, step_coef, image, -1)
                    update(r, r, step_coef, image, -1)
                norm = new
        return carry

    lax.fori_loop(0, steps, time_step, 0)


def solve_grid(nx, ny, steps, layers, tile_x, volts, injected, coef):
    size, width = volts.shape
    halos, grams = steps * (ITERS + 1), steps * ITERS
    dma = pltpu.SemaphoreType.DMA
    return pl.pallas_call(
        functools.partial(grid_kernel, nx, ny, steps, layers, tile_x),
        out_shape=[jax.ShapeDtypeStruct(volts.shape, F32)] * 2,
        in_specs=[pl.BlockSpec(memory_space=pltpu.VMEM)] * 3,
        out_specs=[pl.BlockSpec(memory_space=pltpu.VMEM)] * 2,
        scratch_shapes=[
            pltpu.VMEM(volts.shape, F32),
            pltpu.VMEM(volts.shape, F32),
            pltpu.VMEM((halos, 2, size, layers * LANES), F32),
            pltpu.VMEM((halos, 2, size, layers * LANES), F32),
            pltpu.VMEM((halos, 2, size, LANES), F32),
            pltpu.VMEM((halos, 2, size, LANES), F32),
            pltpu.VMEM((grams, size, LANES), F32),
            pltpu.VMEM((grams, nx, size, LANES), F32),
            pltpu.VMEM((grams, size, LANES), F32),
            pltpu.VMEM((grams, ny, size, LANES), F32),
            dma((halos, 2)), dma((halos, 2)), dma((halos, 2)), dma((halos, 2)),
            dma((grams, nx)), dma((grams, nx)), dma((grams, ny)), dma((grams, ny)),
        ],
        compiler_params=pltpu.CompilerParams(
            collective_id=0, has_side_effects=True, vmem_limit_bytes=48 * 1024 * 1024
        ),
        name="grid",
    )(volts, injected, coef)


def shifted(x, axis):
    length = lax.axis_size(axis)
    return lax.ppermute(x, axis, [(i, i + 1) for i in range(length - 1)])


def body(volts, cap, cond_x, cond_y, via, waveforms, placement, cells, wave_ids, amps):
    nx, ny = lax.axis_size("gx"), lax.axis_size("gy")
    devices = nx * ny
    scenarios, layers, tile_x, tile_y = volts.shape
    steps = waveforms.shape[0] // scenarios
    capacity = 2 * cells.shape[0] // devices
    slots = bin_instances(devices, capacity, placement[:, 0], cells, wave_ids, amps)
    arrived = lax.all_to_all(
        slots.reshape(2, devices, capacity), ("gx", "gy"), split_axis=1, concat_axis=1, tiled=True
    )
    injected = inject(arrived, waveforms, tile_x * tile_y)
    rim_x = shifted(cond_x[:, -1:, :], "gx")
    rim_y = shifted(cond_y[:, :, -1:], "gy")
    x_low = jnp.concatenate([rim_x, cond_x[:, :-1, :]], axis=1)
    y_low = jnp.concatenate([rim_y, cond_y[:, :, :-1]], axis=2)
    via_low = jnp.concatenate([jnp.zeros_like(via[:1]), via[:-1]], axis=0)
    at_x = lax.broadcasted_iota(jnp.int32, cond_x.shape, 1) + lax.axis_index("gx") * tile_x
    at_y = lax.broadcasted_iota(jnp.int32, cond_y.shape, 2) + lax.axis_index("gy") * tile_y
    x_next = jnp.where(at_x == nx * tile_x - 1, 0.0, cond_x)
    y_next = jnp.where(at_y == ny * tile_y - 1, 0.0, cond_y)
    around = cond_x + x_low + cond_y + y_low + via + via_low
    coef = jnp.stack([cap + around, around, x_next, x_low, y_next, y_low, via, via_low])
    coef = coef.reshape(8, layers * tile_x, tile_y)
    out, residual = solve_grid(
        nx, ny, steps, layers, tile_x, volts.reshape(scenarios, -1), injected, coef
    )
    return out.reshape(volts.shape), residual.reshape(volts.shape)


def solution(mesh):
    grid = P(None, "gx", "gy")
    field = P(None, None, "gx", "gy")
    flat = P(("gx", "gy"))
    return jax.shard_map(
        body,
        mesh=mesh,
        in_specs=(field, grid, grid, grid, grid, P(), P(("gx", "gy"), None), flat, flat, flat),
        out_specs=(field, field),
        check_vma=False,
    )
```

time: 658 us -> 177 us (0.27); the launches traced: 648 us -> 176 us
  blocking collectives: 266 us -> 0 us
  Pallas kernels: 0 us -> 145 us
  local copies, waits for them, and re-layouts: 107 us -> 11.4 us
  other arithmetic: 95.1 us -> 0.98 us
  starting transfers between devices: 104 us -> 11.7 us
  matrix products: 68.5 us -> 0 us
    psum x6 -> x0, blocking collectives: 266 us -> none  [the longest x4 174 us: body(): lax.psum((gram(direction, image), gram(residual, image), gram(image, imag...]
    pallas_call x0 -> x3, Pallas kernels: none -> 145 us  [the longest x1 123 us: solve_grid(): pl.pallas_call(functools.partial(grid_kernel, nx, ny, steps, layers, tile...]
    ppermute x34 -> x2, starting transfers between devices: 89.1 us -> 6.67 us  [shifted(): return lax.ppermute(x, axis, [(i, i + 1) for i in range(length - 1)])]
    another operation x52 -> x0, other arithmetic: 78 us -> none  [the longest x30 36.1 us: spd_solve(): factor = jnp.linalg.cholesky(matrix)]
    dot_general x58 -> x0, matrix products: 64.3 us -> none  [the longest x16 42.7 us: add_block(): jnp.dot(piece_values, one_hot, preferred_element_type=jnp.float32)]
    unnamed x79 -> x26, local copies, waits for them, and re-layouts: 40.2 us -> 5.07 us
    scatter x1 -> x0, local copies, waits for them, and re-layouts: 23.7 us -> none  [body(): jnp.zeros((currents.shape[0], slots_all), jnp.bfloat16).at[:, slot_index]]
    slice x42 -> x2, local copies, waits for them, and re-layouts: 16.5 us -> 1.52 us  [the longest x1 0.79 us: body(): rim_y = shifted(cond_y[:, :, -1:], 'gy')]
  transfers between devices with their start and end apart: 36 -> 3, of which waited for: 10 -> 1; matrix products, arithmetic and copies ran while one was open for 10% -> 4% of each run, Pallas kernels for 0% -> 6%
where the time goes in v1:
time: 177 us; the launch traced here: 176 us
  Pallas kernels  145 us (82%)
  starting transfers between devices  11.7 us (7%)
  local copies, waits for them, and re-layouts  11.4 us (6%)
  waiting for transfers between devices  6.64 us (4%)
    pallas_call x1, Pallas kernels, solve_grid(): pl.pallas_call(functools.partial(grid_kernel, nx, ny, steps, layers, tile...  123 us
    pallas_call x1, Pallas kernels, inject(): pl.pallas_call(functools.partial(inject_kernel, parts), out_shape=jax.Sha...  12.3 us
    pallas_call x1, Pallas kernels, bin_instances(): pl.pallas_call(functools.partial(bin_kernel, devices, capacity), out_shap...  9.78 us
    ppermute x2, starting transfers between devices, shifted(): return lax.ppermute(x, axis, [(i, i + 1) for i in range(length - 1)])  6.67 us
    all_to_all x1, waiting for transfers between devices, body(): lax.all_to_all(slots.reshape(2, devices, capacity), ('gx', 'gy'), split_a...  6.63 us
    unnamed x26, local copies, waits for them, and re-layouts  5.07 us
    all_to_all x1, starting transfers between devices, body(): lax.all_to_all(slots.reshape(2, devices, capacity), ('gx', 'gy'), split_a...  5.02 us
  transfers between devices with their start and end apart: 3, of which 1 were waited for; matrix products, arithmetic and copies ran while one was open for 4% of the time, Pallas kernels for 6%

profile of v1, /device:TPU:0, one launch (start us, length us, event | category | flops | bytes accessed | tf_op | source)
XLA Modules:
  0.0 176.1 jit_solution(17816120511334309407)
XLA Ops:
  0.6 0.7 slice.15
  1.4 2.4 %collective-permute-start = (f32[4,1,128]{2,1,0:T(1,128)S(1)}, f32[4,1,128]{2,1,0:T(1,128)S(1)}, u32[]{:S(2)}, u32[]{:S(2)}) collective-permute-start(f32[4,1,128]{2,1,0:T(1,128)S(1)} %slice.15), channel_id=1, source_target_pairs={{0,4},{4,8},{8,12},{12,16},{16,20},{20,24},{24,28},{1,5},{5,9},{9,... | collective-permute-start | bytes 6152 | tf_op jit(solution)/shard_map/ppermute | solution.py:338
  3.8 0.8 slice.17
  4.6 4.3 %collective-permute-start.1 = (f32[4,8,1]{2,1,0:T(8,128)S(1)}, f32[4,8,1]{2,1,0:T(8,128)S(1)}, u32[]{:S(2)}, u32[]{:S(2)}) collective-permute-start(f32[4,8,1]{2,1,0:T(8,128)S(1)} %slice.17), channel_id=1, source_target_pairs={{0,1},{1,2},{2,3},{4,5},{5,6},{6,7},{8,9},{9,10},{10,11},{12,13},{... | collective-permute-start | bytes 392 | tf_op jit(solution)/shard_map/ppermute | solution.py:338
  8.8 0.5 broadcast.13
  9.4 0.7 reduce.3
  10.1 0.6 reshape_squeeze.3.target_ref
  10.7 0.1 copy-done.6
  10.9 0.6 reshape.43.cell_ref
  11.5 0.1 copy-done.7
  11.6 0.6 reshape.44.wave_ref
  12.2 0.2 copy-done.8
  12.4 0.6 reshape.45.amp_ref
  13.0 9.8 %bin.1 = f32[2,128,128]{2,1,0:T(8,128)} custom-call(s32[16,512]{1,0:T(8,128)} %reshape_squeeze.3.target_ref, s32[16,512]{1,0:T(8,128)} %reshape.43.cell_ref, s32[16,512]{1,0:T(8,128)} %reshape.44.wave_ref, f32[16,512]{1,0:T(8,128)} %reshape.45.amp_ref), custom_call_target="tpu_custom_call" | custom-call | tf_op jit(solution)/shard_map/bin/pallas_call | solution.py:66
  22.8 0.9 reshape.46
  23.7 0.8 copy.12
  24.5 5.0 %all-to-all-start = ((f32[2,32,512]{2,0,1:T(2,128)}), f32[2,32,512]{2,0,1:T(2,128)S(1)}, u32[]{:S(2)}, u32[]{:S(2)}) async-start(f32[2,32,512]{2,0,1:T(2,128)} %copy.12), calls=%async_computation | async-start | bytes 262144 | tf_op jit(solution)/shard_map/all_to_all | solution.py:348
  29.5 0.7 copy-done.4
  30.2 0.3 copy.18
  30.6 0.4 copy-done.2
  30.9 0.0 copy-done.3
  30.9 0.0 copy-done.9
  31.0 0.1 constant_dynamic-update-slice_fusion.7
  31.0 0.1 constant_dynamic-update-slice_fusion.5
  31.1 0.1 constant_dynamic-update-slice_fusion.2
  31.2 6.6 %all-to-all-done = f32[2,32,512]{2,0,1:T(2,128)S(1)} async-done(((f32[2,32,512]{2,0,1:T(2,128)}), f32[2,32,512]{2,0,1:T(2,128)S(1)}, u32[]{:S(2)}, u32[]{:S(2)}) %all-to-all-start) | async-done | bytes 131104 | tf_op jit(solution)/shard_map/all_to_all | solution.py:348
  37.9 0.7 copy.13.arrived_ref
  38.5 12.3 %inject.1.inj = f32[64,1024]{1,0:T(8,128)} custom-call(f32[2,32,512]{2,1,0:T(8,128)} %copy.13.arrived_ref, f32[64,64]{1,0:T(8,128)} %wave_ref.1), custom_call_target="tpu_custom_call" | custom-call | tf_op jit(solution)/shard_map/inject/pallas_call | solution.py:107
  50.8 0.9 copy-done
  51.8 122.6 %grid.1 = (f32[32,4096]{1,0:T(8,128)S(1)}, f32[32,4096]{1,0:T(8,128)S(1)}) custom-call(f32[32,4096]{1,0:T(8,128)S(1)} %bitcast.32, f32[64,1024]{1,0:T(8,128)S(1)} %copy-done, f32[8,32,128]{2,1,0:T(8,128)S(1)} %constant_dynamic-update-slice_fusion.coef), custom_call_target="tpu_custom_call" | custom-call | tf_op jit(solution)/shard_map/grid/pallas_call | solution.py:310
  174.3 0.9 copy.15
  175.2 0.9 copy.16
  (22 shorter events, 0.1 us)
Async XLA Ops:
  0.6 8.7 %copy-start.5 = (s32[8192,1]{0,1:T(1,128)S(1)}, s32[8192,1]{0,1:T(1,128)}, u32[]{:S(2)}) copy-start(s32[8192,1]{0,1:T(1,128)} %param.16) | copy-start | bytes 98308
  1.4 29.2 %collective-permute-start = (f32[4,1,128]{2,1,0:T(1,128)S(1)}, f32[4,1,128]{2,1,0:T(1,128)S(1)}, u32[]{:S(2)}, u32[]{:S(2)}) collective-permute-start(f32[4,1,128]{2,1,0:T(1,128)S(1)} %slice.15), channel_id=1, source_target_pairs={{0,4},{4,8},{8,12},{12,16},{16,20},{20,24},{24,28},{1,5},{5,9},{9,... | collective-permute-start | bytes 6152 | tf_op jit(solution)/shard_map/ppermute | solution.py:338
  4.6 26.0 %collective-permute-start.1 = (f32[4,8,1]{2,1,0:T(8,128)S(1)}, f32[4,8,1]{2,1,0:T(8,128)S(1)}, u32[]{:S(2)}, u32[]{:S(2)}) collective-permute-start(f32[4,8,1]{2,1,0:T(8,128)S(1)} %slice.17), channel_id=1, source_target_pairs={{0,1},{1,2},{2,3},{4,5},{5,6},{6,7},{8,9},{9,10},{10,11},{12,13},{... | collective-permute-start | bytes 392 | tf_op jit(solution)/shard_map/ppermute | solution.py:338
  10.1 0.8 copy-start.6
  10.9 0.8 copy-start.7
  11.6 0.8 copy-start.8
  13.0 17.2 %copy-start.1 = (f32[32,4,8,128]{3,2,1,0:T(8,128)S(1)}, f32[32,4,8,128]{3,2,1,0:T(8,128)}, u32[]{:S(2)}) copy-start(f32[32,4,8,128]{3,2,1,0:T(8,128)} %param.10) | copy-start | bytes 1572868
  24.5 13.4 %all-to-all-start = ((f32[2,32,512]{2,0,1:T(2,128)}), f32[2,32,512]{2,0,1:T(2,128)S(1)}, u32[]{:S(2)}, u32[]{:S(2)}) async-start(f32[2,32,512]{2,0,1:T(2,128)} %copy.12), calls=%async_computation | async-start | bytes 262144 | tf_op jit(solution)/shard_map/all_to_all | solution.py:348
  29.5 0.7 copy-start.4
  30.2 0.7 copy-start.2
  30.2 0.7 copy-start.3
  30.2 0.7 copy-start.9
  50.8 0.9 copy-start
